TPU v7x, 32 devices: a whole 2x2x4 slice. The times are simulated.
32 devices in a mesh: cells: 8 (over y, x, core), genes: 4 (over z).
Axes of the slice: x: 2, y: 2, z: 4, core: 2. Of those that a mesh axis runs over, the one named last changes fastest.
Arguments:
- counts: int32 [8192, 4096], P('cells', 'genes'), may hold values from 0 to 26, as said below
- library: int32 [8192], P('cells'), may hold values from 2000 to 19999
Outputs:
- adjacency: float32 [4096, 4096], P('cells', 'genes')
- connectivity: float32 [4096], P('cells')
Inputs may be any that keep to these rules, and one draw needn't show every extreme that they name: Non-negative integer counts.
All inputs are finite; a program needn't handle non-finite values.
Results may differ from a plain program's by a relative error of at most 0.006.
Values may be sent and summed in bfloat16 or wider, within the bound.
A program may use at most 128 MiB of HBM per device.

v0:
```python
import jax
import jax.numpy as jnp
from jax import lax
from jax.sharding import PartitionSpec as P


def normalize(counts, library):
    factor = 10000.0 / library.astype(jnp.float32)
    return jnp.log1p(counts.astype(jnp.float32) * factor[:, None]).astype(jnp.bfloat16)


def cross_product(left, right):
    return lax.dot_general(
        left, right, (((0,), (0,)), ((), ())), preferred_element_type=jnp.float32
    )


def shards(counts, library):
    own_block = normalize(counts, library)
    col_width = own_block.shape[1]
    cell_groups = lax.axis_size("cells")
    gene_total = col_width * lax.axis_size("genes")
    row_width = gene_total // cell_groups
    total_cells = float(counts.shape[0] * cell_groups)
    widened = own_block.astype(jnp.float32)
    local_sums = jnp.sum(widened, axis=0)
    local_squares = jnp.sum(widened * widened, axis=0)
    block_sums, block_squares = lax.psum((local_sums, local_squares), "cells")
    gene_sums, gene_squares = (
        lax.all_gather(block_sums, "genes", axis=0, tiled=True),
        lax.all_gather(block_squares, "genes", axis=0, tiled=True),
    )
    full_block = lax.all_gather(own_block, "genes", axis=1, tiled=True)
    gram_tile = lax.psum_scatter(
        cross_product(full_block, own_block), "cells", scatter_dimension=0, tiled=True
    )
    means = gene_sums / total_cells
    variances = gene_squares / total_cells - means * means
    scales = lax.rsqrt(variances + 1e-05)
    row_first = lax.axis_index("cells") * row_width
    col_first = lax.axis_index("genes") * col_width
    row_means = lax.dynamic_slice_in_dim(means, row_first, row_width, 0)
    col_means = lax.dynamic_slice_in_dim(means, col_first, col_width, 0)
    row_scales = lax.dynamic_slice_in_dim(scales, row_first, row_width, 0)
    col_scales = lax.dynamic_slice_in_dim(scales, col_first, col_width, 0)
    correlation = (
        (gram_tile / total_cells - row_means[:, None] * col_means[None, :])
        * row_scales[:, None]
        * col_scales[None, :]
    )
    powered = correlation**6
    row_index = row_first + jnp.arange(row_width, dtype=jnp.int32)[:, None]
    col_index = col_first + jnp.arange(col_width, dtype=jnp.int32)[None, :]
    adjacency = jnp.where(row_index == col_index, jnp.float32(0.0), powered)
    connectivity = lax.psum(jnp.sum(adjacency, axis=1), "genes")
    return (adjacency, connectivity)


def solution(mesh):
    return jax.shard_map(
        shards,
        mesh=mesh,
        in_specs=(P("cells", "genes"), P("cells")),
        out_specs=(P("cells", "genes"), P("cells")),
        check_vma=False,
    )
```

profile of v0, /device:TPU:0, one launch (start us, length us, event | category | flops | bytes accessed | tf_op | source)
XLA Modules:
  0.0 318.0 jit_solution(6613592547870994486)
XLA Ops:
  7.2 0.0 all-gather.2.cloned.1.call-start
  7.2 0.7 convert_divide_fusion
  7.9 5.6 %convert_reduce_fusion = (f32[1024]{0:T(1024)S(1)}, f32[1024]{0:T(1024)S(1)}, bf16[1024,1024]{1,0:T(8,128)(2,1)}) fusion(f32[1024]{0:T(1024)S(1)} %convert_divide_fusion, s32[1024,1024]{1,0:T(8,128)} %param.2), kind=kLoop, calls=%fused_computation.1 | loop fusion | flops 7337984 | bytes 6303744 | tf_op jit(solution)/shard_map/reduce_sum | solution.py:26
  13.5 0.0 copy-start
  13.5 0.0 all-gather.2.cloned.1.call-update
  13.5 0.0 reduce-scatter.2.cloned.1.call-start
  13.5 152.4 %all-gather.2.cloned.1.call-done = bf16[1024,4096]{1,0:T(8,128)(2,1)} async-done(((bf16[1024,1024]{1,0:T(8,128)(2,1)}), bf16[1024,4096]{1,0:T(8,128)(2,1)}) %all-gather.2.cloned.1.call-update) | async-done | bytes 8388624 | tf_op jit(solution)/shard_map/all_gather | solution.py:33
  166.0 0.0 copy-done
  166.0 14.6 %fusion.4 = f32[4096,1024]{1,0:T(8,128)} fusion(bf16[1024,4096]{1,0:T(8,128)(2,1)} %all-gather.2.cloned.1.call-done, bf16[1024,1024]{1,0:T(8,128)(2,1)S(1)} %copy-done), kind=kOutput, calls=%fused_computation.12 | convolution fusion | flops 8589934592 | bytes 27262976 | tf_op jit(solution)/shard_map/dot_general | solution.py:13
  180.6 0.0 reduce-scatter.2.cloned.1.call-update
  180.7 14.0 %all-reduce = (f32[1024]{0:T(1024)S(1)}, f32[1024]{0:T(1024)S(1)}) all-reduce(f32[1024]{0:T(1024)S(1)} %get-tuple-element.3, f32[1024]{0:T(1024)S(1)} %get-tuple-element.2), channel_id=1, replica_groups=mesh['cells'=8,'genes'=4] {'cells'}, use_global_device_ids=true, to_apply=%region_4.0 | all-reduce | flops 2048 | bytes 16384 | tf_op jit(solution)/shard_map/psum | solution.py:28
  194.7 13.2 %all_gather.10 = f32[4096]{0:T(1024)S(1)} all-gather(f32[1024]{0:T(1024)S(1)} %get-tuple-element.5), channel_id=1, replica_groups=mesh['cells'=8,'genes'=4] {'genes'}, dimensions={0}, use_global_device_ids=true | all-gather | bytes 20480 | tf_op jit(solution)/shard_map/all_gather | solution.py:30
  207.9 13.2 %all_gather.11 = f32[4096]{0:T(1024)S(1)} all-gather(f32[1024]{0:T(1024)S(1)} %get-tuple-element.4), channel_id=1, replica_groups=mesh['cells'=8,'genes'=4] {'genes'}, dimensions={0}, use_global_device_ids=true | all-gather | bytes 20480 | tf_op jit(solution)/shard_map/all_gather | solution.py:31
  221.1 0.1 dynamic_slice.12
  221.2 0.1 dynamic_slice.14
  221.3 73.9 %reduce-scatter.2.cloned.1.call-done = f32[512,1024]{1,0:T(8,128)} async-done(((f32[4096,1024]{1,0:T(8,128)}), f32[512,1024]{1,0:T(8,128)}) %reduce-scatter.2.cloned.1.call-update) | async-done | bytes 2097168 | tf_op jit(solution)/shard_map/reduce_scatter | solution.py:34
  295.2 3.8 %fusion.2 = (f32[512]{0:T(512)S(1)}, f32[512,1024]{1,0:T(8,128)}) fusion(f32[1024]{0:T(1024)S(1)} %dynamic_slice.15, f32[512]{0:T(512)S(1)} %dynamic_slice.14, f32[1024]{0:T(1024)S(1)} %dynamic_slice.13, f32[512]{0:T(512)S(1)} %dynamic_slice.12, f32[512,1024]{1,0:T(8,128)} %reduce-scatter.2.cloned.1.call-done, s32[1024]{0:T(1024)S(1)} %iota_add_fusion, ...), kind=kLoop, calls=%fused_computation.11 | loop fusion | flops 5766656 | bytes 4214784 | tf_op jit(solution)/shard_map/reduce_sum | solution.py:55
  299.0 12.2 %psum.23 = f32[512]{0:T(512)} all-reduce(f32[512]{0:T(512)S(1)} %get-tuple-element.6), channel_id=1, replica_groups=mesh['cells'=8,'genes'=4] {'genes'}, use_global_device_ids=true, to_apply=%region_6.7 | all-reduce | flops 512 | bytes 4096 | tf_op jit(solution)/shard_map/psum | solution.py:55
  (5 shorter events, 0.0 us)
Async XLA Ops:
  7.2 158.8 %all-gather.2.cloned.1.call-start = ((), (), s32[]{:S(2)}) async-start(), calls=%async_computation.1 | async-start | bytes 10485760 | tf_op jit(solution)/shard_map/all_gather | solution.py:33
  13.5 152.5 %copy-start = (bf16[1024,1024]{1,0:T(8,128)(2,1)S(1)}, bf16[1024,1024]{1,0:T(8,128)(2,1)}, u32[]{:S(2)}) copy-start(bf16[1024,1024]{1,0:T(8,128)(2,1)} %get-tuple-element.8) | copy-start | bytes 6291460
  13.5 281.7 %reduce-scatter.2.cloned.1.call-start = ((), (), s32[]{:S(2)}) async-start(), calls=%async_computation.2 | async-start | bytes 18874368 | tf_op jit(solution)/shard_map/reduce_scatter | solution.py:34
Sparse Core Ops, SparseCore 0:
  13.6 152.3 all-gather.1
  180.8 114.3 reduce-scatter.1
where the time goes:
time: 318 us
  waiting for transfers between devices  226 us (71%)
  blocking collectives  52.7 us (17%)
  matrix products  14.6 us (5%)
  between operations  14.1 us (4%)
  other arithmetic  10 us (3%)
    all_gather x1, waiting for transfers between devices, shards(): full_block = lax.all_gather(own_block, 'genes', axis=1, tiled=True)  152 us
    reduce_scatter x1, waiting for transfers between devices, shards(): lax.psum_scatter(cross_product(full_block, own_block), 'cells', scatter_d...  73.9 us
    dot_general x1, matrix products, cross_product(): lax.dot_general(left, right, (((0,), (0,)), ((), ())), preferred_element_...  14.6 us
    psum x1, blocking collectives, shards(): block_sums, block_squares = lax.psum((local_sums, local_squares), 'cells')  14 us
    all_gather x1, blocking collectives, shards(): lax.all_gather(block_sums, 'genes', axis=0, tiled=True)  13.2 us
    all_gather x1, blocking collectives, shards(): lax.all_gather(block_squares, 'genes', axis=0, tiled=True)  13.2 us
    psum x1, blocking collectives, shards(): connectivity = lax.psum(jnp.sum(adjacency, axis=1), 'genes')  12.2 us
  transfers between devices with their start and end apart: 2, of which 2 were waited for; matrix products, arithmetic and copies ran while one was open for 0% of the time, Pallas kernels for 0%

commit v1 on v0

--- a/solution.py
+++ b/solution.py
@@ -30,7 +30,10 @@
         lax.all_gather(block_sums, "genes", axis=0, tiled=True),
         lax.all_gather(block_squares, "genes", axis=0, tiled=True),
     )
-    full_block = lax.all_gather(own_block, "genes", axis=1, tiled=True)
+    taken_in = lax.axis_size("genes")
+    full_block = jnp.concatenate(
+        lax.all_to_all(jnp.stack(taken_in * [own_block]), "genes", 0, 0), axis=1
+    )
     gram_tile = lax.psum_scatter(
         cross_product(full_block, own_block), "cells", scatter_dimension=0, tiled=True
     )

time: 318 us -> 358 us (1.13)
  blocking collectives: 52.7 us -> 241 us
  waiting for transfers between devices: 226 us -> 76.5 us
  local copies, waits for them, and re-layouts: 0.17 us -> 4.22 us
    all_to_all x0 -> x1, blocking collectives: none -> 189 us  [shards(): lax.all_to_all(jnp.stack(taken_in * [own_block]), 'genes', 0, 0)]
    all_gather x1 -> x0, waiting for transfers between devices: 152 us -> none  [shards(): full_block = lax.all_gather(own_block, 'genes', axis=1, tiled=True)]
  transfers between devices with their start and end apart: 2 -> 1, of which waited for: 2 -> 1; matrix products, arithmetic and copies ran while one was open for 0% -> 0% of each run, Pallas kernels for 0% -> 0%
where the time goes in v1:
time: 358 us; the launch traced here: 357 us
  blocking collectives  241 us (67%)
  waiting for transfers between devices  76.5 us (21%)
  between operations  14.1 us (4%)
  matrix products  11.6 us (3%)
  other arithmetic  10 us (3%)
  local copies, waits for them, and re-layouts  4.22 us (1%)
    all_to_all x1, blocking collectives, shards(): lax.all_to_all(jnp.stack(taken_in * [own_block]), 'genes', 0, 0)  189 us
    reduce_scatter x1, waiting for transfers between devices, shards(): lax.psum_scatter(cross_product(full_block, own_block), 'cells', scatter_d...  76.5 us
    all_gather x1, blocking collectives, shards(): lax.all_gather(block_sums, 'genes', axis=0, tiled=True)  13.2 us
    all_gather x1, blocking collectives, shards(): lax.all_gather(block_squares, 'genes', axis=0, tiled=True)  13.2 us
    psum x1, blocking collectives, shards(): block_sums, block_squares = lax.psum((local_sums, local_squares), 'cells')  12.8 us
    psum x1, blocking collectives, shards(): connectivity = lax.psum(jnp.sum(adjacency, axis=1), 'genes')  12.2 us
    dot_general x1, matrix products, cross_product(): lax.dot_general(left, right, (((0,), (0,)), ((), ())), preferred_element_...  11.6 us
  transfers between devices with their start and end apart: 1, of which 1 were waited for; matrix products, arithmetic and copies ran while one was open for 0% of the time, Pallas kernels for 0%

profile of v1, /device:TPU:0, one launch (start us, length us, event | category | flops | bytes accessed | tf_op | source)
XLA Modules:
  0.0 357.4 jit_solution(1155195627973683603)
XLA Ops:
  7.2 0.0 reduce-scatter.2.cloned.1.call-start
  7.2 0.7 convert_divide_fusion
  7.9 5.6 %convert_reduce_fusion = (f32[1024]{0:T(1024)S(1)}, f32[1024]{0:T(1024)S(1)}, bf16[1024,1024]{1,0:T(8,128)(2,1)}) fusion(f32[1024]{0:T(1024)S(1)} %convert_divide_fusion, s32[1024,1024]{1,0:T(8,128)} %param.2), kind=kLoop, calls=%fused_computation.1 | loop fusion | flops 7337984 | bytes 6303744 | tf_op jit(solution)/shard_map/reduce_sum | solution.py:26
  13.5 2.9 copy.5
  16.3 1.2 stack.2
  17.5 0.0 copy-start
  17.5 189.3 %all_to_all.5 = bf16[4,1024,1024]{1,2,0:T(8,128)(2,1)S(1)} all-to-all(bf16[4,1024,1024]{1,2,0:T(8,128)(2,1)S(1)} %stack.2), channel_id=1, replica_groups=mesh['cells'=8,'genes'=4] {'genes'}, dimensions={0} | all-to-all | bytes 16777216 | tf_op jit(solution)/shard_map/all_to_all | solution.py:35
  206.8 0.0 copy-done
  206.8 11.6 %fusion.4 = f32[4096,1024]{1,0:T(8,128)} fusion(bf16[1024,4096]{0,1:T(8,128)(2,1)S(1)} %bitcast.5, bf16[1024,1024]{1,0:T(8,128)(2,1)S(1)} %copy-done), kind=kOutput, calls=%fused_computation.12 | convolution fusion | flops 8589934592 | bytes 27262976 | tf_op jit(solution)/shard_map/dot_general | solution.py:13
  218.5 0.0 reduce-scatter.2.cloned.1.call-update
  218.5 12.8 %all-reduce = (f32[1024]{0:T(1024)S(1)}, f32[1024]{0:T(1024)S(1)}) all-reduce(f32[1024]{0:T(1024)S(1)} %get-tuple-element.3, f32[1024]{0:T(1024)S(1)} %get-tuple-element.2), channel_id=1, replica_groups=mesh['cells'=8,'genes'=4] {'cells'}, use_global_device_ids=true, to_apply=%region_4.0 | all-reduce | flops 2048 | bytes 16384 | tf_op jit(solution)/shard_map/psum | solution.py:28
  231.4 13.2 %all_gather.6 = f32[4096]{0:T(1024)S(1)} all-gather(f32[1024]{0:T(1024)S(1)} %get-tuple-element.5), channel_id=1, replica_groups=mesh['cells'=8,'genes'=4] {'genes'}, dimensions={0}, use_global_device_ids=true | all-gather | bytes 20480 | tf_op jit(solution)/shard_map/all_gather | solution.py:30
  244.6 13.2 %all_gather.7 = f32[4096]{0:T(1024)S(1)} all-gather(f32[1024]{0:T(1024)S(1)} %get-tuple-element.4), channel_id=1, replica_groups=mesh['cells'=8,'genes'=4] {'genes'}, dimensions={0}, use_global_device_ids=true | all-gather | bytes 20480 | tf_op jit(solution)/shard_map/all_gather | solution.py:31
  257.8 0.1 dynamic_slice.12
  257.9 0.1 dynamic_slice.14
  258.0 76.5 %reduce-scatter.2.cloned.1.call-done = f32[512,1024]{1,0:T(8,128)} async-done(((f32[4096,1024]{1,0:T(8,128)}), f32[512,1024]{1,0:T(8,128)}) %reduce-scatter.2.cloned.1.call-update) | async-done | bytes 2097168 | tf_op jit(solution)/shard_map/reduce_scatter | solution.py:37
  334.5 3.8 %fusion.2 = (f32[512]{0:T(512)S(1)}, f32[512,1024]{1,0:T(8,128)}) fusion(f32[1024]{0:T(1024)S(1)} %dynamic_slice.15, f32[512]{0:T(512)S(1)} %dynamic_slice.14, f32[1024]{0:T(1024)S(1)} %dynamic_slice.13, f32[512]{0:T(512)S(1)} %dynamic_slice.12, f32[512,1024]{1,0:T(8,128)} %reduce-scatter.2.cloned.1.call-done, s32[1024]{0:T(1024)S(1)} %iota_add_fusion, ...), kind=kLoop, calls=%fused_computation.11 | loop fusion | flops 5766656 | bytes 4214784 | tf_op jit(solution)/shard_map/reduce_sum | solution.py:58
  338.3 12.2 %psum.23 = f32[512]{0:T(512)} all-reduce(f32[512]{0:T(512)S(1)} %get-tuple-element.6), channel_id=1, replica_groups=mesh['cells'=8,'genes'=4] {'genes'}, use_global_device_ids=true, to_apply=%region_6.7 | all-reduce | flops 512 | bytes 4096 | tf_op jit(solution)/shard_map/psum | solution.py:58
  (5 shorter events, 0.0 us)
Async XLA Ops:
  7.2 327.4 %reduce-scatter.2.cloned.1.call-start = ((), (), s32[]{:S(2)}) async-start(), calls=%async_computation.2 | async-start | bytes 18874368 | tf_op jit(solution)/shard_map/reduce_scatter | solution.py:37
  17.5 189.3 %copy-start = (bf16[1024,1024]{1,0:T(8,128)(2,1)S(1)}, bf16[1024,1024]{1,0:T(8,128)(2,1)}, u32[]{:S(2)}) copy-start(bf16[1024,1024]{1,0:T(8,128)(2,1)} %get-tuple-element.8) | copy-start | bytes 6291460
Sparse Core Ops, SparseCore 0:
  218.6 115.8 reduce-scatter.1
